TPU v7x, 32 devices: a whole 2x2x4 slice. The times are simulated.
32 devices in a mesh: tp: 4 (over x, core), fsdp: 8 (over z, y).
Axes of the slice: x: 2, y: 2, z: 4, core: 2. Of those that a mesh axis runs over, the one named last changes fastest.
Arguments:
- sectioned: bfloat16 [64, 256, 26624], P('fsdp', None, 'tp'), as said below
- loader_owner: int32 [64], replicated, may hold values from 0 to 7, as said below
- slab_order: int32 [64], replicated, may hold values from 0 to 7, as said below
Outputs:
- dequant: bfloat16 [16384, 26624], P(('tp', 'fsdp'))
- scale_codes: float32 [26624, 256], P(('tp', 'fsdp'))
- group_max: float32 [26624], P(('tp', 'fsdp'))
Inputs may be any that keep to these rules, and one draw needn't show every extreme that they name: `loader_owner`: slab s holds rows s * 256 to (s + 1) * 256 - 1; for each f, the 8 slabs s with (s // 2) % 8 == f have 8 distinct owners. `slab_order`: the slabs of one owner have distinct orders. `sectioned`: entries are finite.
All inputs are finite; a program needn't handle non-finite values. Where the computation divides by a largest or mean magnitude, that divisor is 1e-20 or more.
Results may differ from a plain program's by a relative error of at most 0.0015.
Values may be sent and summed in bfloat16 or wider, within the bound.
A program may use at most 256 MiB of HBM per device.

v0:
```python
import functools

import jax
import jax.numpy as jnp
import numpy as np
from jax import lax
from jax.experimental import pallas as pl
from jax.experimental.pallas import tpu as pltpu
from jax.sharding import PartitionSpec as P

LEVELS = [
    -1.0,
    -0.6961928009986877,
    -0.5250730514526367,
    -0.39491748809814453,
    -0.28444138169288635,
    -0.18477343022823334,
    -0.09105003625154495,
    0.0,
    0.07958029955625534,
    0.16093020141124725,
    0.24611230194568634,
    0.33791524171829224,
    0.44070982933044434,
    0.5626170039176941,
    0.7229568362236023,
    1.0,
]
MIDPOINTS = [(LEVELS[k] + LEVELS[k + 1]) / 2.0 for k in range(15)]
STEPSIZES = [LEVELS[k + 1] - LEVELS[k] for k in range(15)]
EPS = 1e-06
LANES = 128
BLOCK = 64
MESH = pl.DeviceIdType.MESH


def reached_levels():
    total = np.float32(LEVELS[0])
    reached = [float(total)]
    for step in STEPSIZES:
        total = np.float32(total + np.float32(step))
        reached.append(float(total))
    return reached


REACHED = reached_levels()


def code_tile(w):
    lane = lax.broadcasted_iota(jnp.int32, w.shape, 1)
    top = jnp.abs(w)
    low = lane < BLOCK
    first = jnp.broadcast_to(jnp.max(jnp.where(low, top, 0.0), axis=1, keepdims=True), w.shape)
    second = jnp.broadcast_to(jnp.max(jnp.where(low, 0.0, top), axis=1, keepdims=True), w.shape)
    spread = jnp.where(lane < BLOCK, first, second)
    ratio = w / (spread + EPS)
    level = jnp.full(w.shape, REACHED[0], jnp.float32)
    for middle, value in zip(MIDPOINTS, REACHED[1:]):
        level = jnp.where(ratio > middle, value, level)
    return spread * level, first, second


def exchange(
    sizes, from_owner, outgoing, out, scales, sums, arrive, coded, tops, s1, r1, l1, s2, r2, l2, sa, ra, la,
    mine, ours, got, met, sm, rm, so, ro, stage,
):
    owners, tp, chunks, rows, per_block, columns, depth = sizes
    t = lax.axis_index("tp")
    f = lax.axis_index("fsdp")
    groups = columns // LANES
    width = next(u for u in range(13, 0, -1) if groups % u == 0)

    barrier = pltpu.get_barrier_semaphore()
    for d in range(1, owners):
        pl.semaphore_signal(barrier, inc=1, device_id={"fsdp": lax.rem(f + d, owners)}, device_id_type=MESH)
    for e in range(1, tp):
        pl.semaphore_signal(barrier, inc=1, device_id={"tp": lax.rem(t + e, tp)}, device_id_type=MESH)
    pl.semaphore_wait(barrier, owners - 1 + tp - 1)

    def span(c):
        return pl.ds(pl.multiple_of(c * rows, rows), rows)

    def first_hop(c, d):
        to = lax.rem(f + d, owners)
        return pltpu.make_async_remote_copy(
            src_ref=outgoing.at[to, span(c)],
            dst_ref=arrive.at[c, f],
            send_sem=s1.at[c, d],
            recv_sem=r1.at[c, d],
            device_id={"fsdp": to},
            device_id_type=MESH,
        )

    def first_stay(c):
        return pltpu.make_async_copy(outgoing.at[f, span(c)], arrive.at[c, f], l1.at[c])

    def start_chunk(c):
        for d in range(1, owners):
            first_hop(c, d).start()
        first_stay(c).start()

    def second_hop(c, slot, e):
        to = lax.rem(t + e, tp)
        band = pl.ds(pl.multiple_of(t * columns, LANES), columns)
        data = pltpu.make_async_remote_copy(
            src_ref=coded.at[slot, to],
            dst_ref=out.at[:, span(c), band],
            send_sem=s2.at[slot, e],
            recv_sem=r2.at[c, e],
            device_id={"tp": to},
            device_id_type=MESH,
        )
        top = pltpu.make_async_remote_copy(
            src_ref=tops.at[to, :, span(c)],
            dst_ref=scales.at[t, :, span(c)],
            send_sem=sa.at[slot, e],
            recv_sem=ra.at[c, e],
            device_id={"tp": to},
            device_id_type=MESH,
        )
        return data, top

    def second_stay(c, slot):
        band = pl.ds(pl.multiple_of(t * columns, LANES), columns)
        data = pltpu.make_async_copy(coded.at[slot, t], out.at[:, span(c), band], l2.at[slot])
        top = pltpu.make_async_copy(tops.at[t, :, span(c)], scales.at[t, :, span(c)], la.at[slot])
        return data, top

    def drain(c, slot):
        for e in range(1, tp):
            for copy in second_hop(c, slot, e):
                copy.wait_send()
        for copy in second_stay(c, slot):
            copy.wait()

    def code(c, slot, to):
        lane = lax.broadcasted_iota(jnp.int32, (rows, LANES), 1)

        def place(k, _):
            owner = from_owner[to * per_block + k]

            def step(g, held):
                at = pl.multiple_of(g * (width * LANES), width * LANES)
                w = stage[owner, :, pl.ds(at, width * LANES)].astype(jnp.float32)
                made = []
                for j in range(width):
                    value, first, second = code_tile(w[:, j * LANES : (j + 1) * LANES])
                    made.append(value.astype(jnp.bfloat16))
                    index = 2 * (g * width + j)
                    held = jnp.where(lane == index, first, jnp.where(lane == index + 1, second, held))
                coded[slot, to, k, :, pl.ds(at, width * LANES)] = jnp.concatenate(made, axis=1)
                return held

            held = lax.fori_loop(0, groups // width, step, jnp.zeros((rows, LANES), jnp.float32))
            tops[to, k, span(c), :] = held
            mine[...] += held
            return 0

        lax.fori_loop(0, per_block, place, 0)

    def sum_hop(d):
        return pltpu.make_async_remote_copy(
            src_ref=mine,
            dst_ref=got.at[d],
            send_sem=sm.at[d],
            recv_sem=rm.at[d],
            device_id={"fsdp": lax.rem(f + d, owners)},
            device_id_type=MESH,
        )

    def sum_turn(e):
        return pltpu.make_async_remote_copy(
            src_ref=ours,
            dst_ref=met.at[e],
            send_sem=so.at[e],
            recv_sem=ro.at[e],
            device_id={"tp": lax.rem(t + e, tp)},
            device_id_type=MESH,
        )

    for c in range(min(depth, chunks)):
        start_chunk(c)
    mine[...] = jnp.zeros_like(mine)

    def chunk(c, _):
        slot = lax.rem(c, 2)
        for d in range(1, owners):
            first_hop(c, d).wait_recv()
        first_stay(c).wait()

        @pl.when(c + depth < chunks)
        def _():
            start_chunk(c + depth)

        @pl.when(c >= 2)
        def _():
            drain(c - 2, slot)

        def take(o, _):
            stage[o] = arrive[c, o]
            return 0

        lax.fori_loop(0, owners, take, 0)
        for e in range(1, tp + 1):
            code(c, slot, lax.rem(t + e, tp))
            if e > 1:
                for copy in second_hop(c, slot, e - 1):
                    copy.start()
        for copy in second_stay(c, slot):
            copy.start()
        return 0

    lax.fori_loop(0, chunks, chunk, 0)

    if chunks > 1:
        drain(chunks - 2, chunks % 2)
    for d in range(1, owners):
        sum_hop(d).start()
    drain(chunks - 1, (chunks - 1) % 2)
    for d in range(1, owners):
        sum_hop(d).wait()
    total = mine[...]
    for d in range(1, owners):
        total = total + got[d]
    ours[...] = total

    def finish(c, _):
        for d in range(1, owners):
            first_hop(c, d).wait_send()
        for e in range(1, tp):
            for copy in second_hop(c, 0, e):
                copy.wait_recv()
        return 0

    lax.fori_loop(0, chunks, finish, 0)
    for e in range(1, tp):
        sum_turn(e).start()
    for e in range(1, tp):
        sum_turn(e).wait()
    total = ours[...]
    for e in range(1, tp):
        total = total + met[e]
    sums[...] = total


def copy_block(*refs):
    refs[-1][...] = refs[-2][...]


def pick_slots(sectioned, send_slot):
    slots, slab_rows, columns = sectioned.shape
    rows = min(128, slab_rows)
    return pl.pallas_call(
        copy_block,
        grid_spec=pltpu.PrefetchScalarGridSpec(
            num_scalar_prefetch=1,
            grid=(slots, slab_rows // rows),
            in_specs=[pl.BlockSpec((1, rows, columns), lambda i, r, slot: (slot[i], r, 0))],
            out_specs=pl.BlockSpec((1, rows, columns), lambda i, r, slot: (i, r, 0)),
        ),
        out_shape=jax.ShapeDtypeStruct(sectioned.shape, sectioned.dtype),
        name="pick_slots",
    )(send_slot, sectioned)


def settle(values):
    total, columns = values.shape
    rows = next(r for r in (32, 16, 8) if total % r == 0)
    return pl.pallas_call(
        copy_block,
        grid=(total // rows,),
        in_specs=[pl.BlockSpec((rows, columns), lambda i: (i, 0))],
        out_specs=pl.BlockSpec((rows, columns), lambda i: (i, 0)),
        out_shape=jax.ShapeDtypeStruct(values.shape, values.dtype),
        name="settle",
    )(values)


def per_device(sectioned, loader_owner, slab_order):
    owners = lax.axis_size("fsdp")
    tp = lax.axis_size("tp")
    myself = lax.axis_index("fsdp")
    slots, slab_rows, columns = sectioned.shape
    slab_count = loader_owner.shape[0]
    per_block = owners // tp
    slab_ids = jnp.arange(slab_count, dtype=jnp.int32)
    target = slab_ids // per_block % owners
    held = loader_owner == myself
    place = jnp.arange(owners, dtype=jnp.int32)
    picks = (target[None, :] == place[:, None]) & held[None, :]
    send_slot = jnp.sum(jnp.where(picks, slab_order[None, :], 0), axis=1)
    wanted = (place // per_block * owners + myself) * per_block + place % per_block
    sought = wanted[:, None] == slab_ids[None, :]
    from_owner = jnp.sum(jnp.where(sought, loader_owner[None, :], 0), axis=1)

    outgoing = pick_slots(sectioned, send_slot)
    rows = min(16, slab_rows)
    chunks = slab_rows // rows
    blocks = columns // BLOCK
    sizes = (owners, tp, chunks, rows, per_block, columns, 4)
    dma = pltpu.SemaphoreType.DMA
    anywhere = pl.BlockSpec(memory_space=pl.ANY)
    coded, scales, sums = pl.pallas_call(
        functools.partial(exchange, sizes),
        out_shape=(
            jax.ShapeDtypeStruct((per_block, slab_rows, tp * columns), jnp.bfloat16),
            jax.ShapeDtypeStruct((tp, per_block, slab_rows, LANES), jnp.float32),
            jax.ShapeDtypeStruct((rows, LANES), jnp.float32),
        ),
        in_specs=[pl.BlockSpec(memory_space=pltpu.SMEM), anywhere],
        out_specs=(anywhere, anywhere, pl.BlockSpec(memory_space=pltpu.VMEM)),
        scratch_shapes=[
            pltpu.VMEM((chunks, owners, rows, columns), jnp.bfloat16),
            pltpu.VMEM((2, tp, per_block, rows, columns), jnp.bfloat16),
            pltpu.VMEM((tp, per_block, slab_rows, LANES), jnp.float32),
            dma((chunks, owners)),
            dma((chunks, owners)),
            dma((chunks,)),
            dma((2, tp)),
            dma((chunks, tp)),
            dma((2,)),
            dma((2, tp)),
            dma((chunks, tp)),
            dma((2,)),
            pltpu.VMEM((rows, LANES), jnp.float32),
            pltpu.VMEM((rows, LANES), jnp.float32),
            pltpu.VMEM((owners, rows, LANES), jnp.float32),
            pltpu.VMEM((tp, rows, LANES), jnp.float32),
            dma((owners,)),
            dma((owners,)),
            dma((tp,)),
            dma((tp,)),
            pltpu.VMEM((owners, rows, columns), jnp.bfloat16),
        ],
        compiler_params=pltpu.CompilerParams(
            collective_id=0, has_side_effects=True, vmem_limit_bytes=56 * 1024 * 1024
        ),
        name="exchange",
    )(from_owner, outgoing)
    dequant = settle(coded.reshape(per_block * slab_rows, tp * columns))
    absmax = jnp.transpose(scales[..., :blocks], (1, 2, 0, 3)).reshape(-1, 256)
    offset = jnp.sum(sums) / float(slab_count * slab_rows * tp * blocks)
    centred = absmax - offset
    group_max = jnp.max(jnp.abs(centred), axis=1)
    scale_codes = centred / (group_max[:, None] + EPS)
    return (dequant, scale_codes, group_max)


def solution(mesh):
    return jax.shard_map(
        per_device,
        mesh=mesh,
        in_specs=(P("fsdp", None, "tp"), P(), P()),
        out_specs=(P(("tp", "fsdp"), None), P(("tp", "fsdp"), None), P(("tp", "fsdp"))),
        check_vma=False,
    )
```

profile of v0, /device:TPU:13, one launch (start us, length us, event | category | flops | bytes accessed | tf_op | source)
XLA Modules:
  0.0 694.9 jit_solution(7989841770264730887)
XLA Ops:
  0.6 0.7 broadcast_compare_fusion
  1.3 1.3 select_reduce_fusion.1.from_owner
  2.7 1.3 select_reduce_fusion.refs_0_
  3.9 24.2 %pick_slots.1.outgoing = bf16[8,256,6656]{2,1,0:T(8,128)(2,1)} custom-call(s32[8]{0:T(128)} %select_reduce_fusion.refs_0_, bf16[8,256,6656]{2,1,0:T(8,128)(2,1)} %refs_1_.1), custom_call_target="tpu_custom_call" | custom-call | tf_op jit(solution)/shard_map/pick_slots/pallas_call | solution.py:253
  28.2 637.5 %exchange.1 = (bf16[2,256,26624]{2,1,0:T(8,128)(2,1)}, f32[4,2,256,128]{3,2,1,0:T(8,128)}, f32[16,128]{1,0:T(8,128)}) custom-call(s32[8]{0:T(128)} %select_reduce_fusion.1.from_owner, bf16[8,256,6656]{2,1,0:T(8,128)(2,1)} %pick_slots.1.outgoing), custom_call_target="tpu_custom_call" | custom-call | tf_op jit(solution)/shard_map/exchange/pallas_call | solution.py:303
  665.7 1.3 reduce_sum.29
  667.7 0.0 copy-start
  667.7 23.6 %settle.1 = bf16[512,26624]{1,0:T(8,128)(2,1)} custom-call(bf16[512,26624]{1,0:T(8,128)(2,1)} %bitcast.3), custom_call_target="tpu_custom_call" | custom-call | tf_op jit(solution)/shard_map/settle/pallas_call | solution.py:269
  691.3 0.0 copy-done
  691.3 0.1 subtract_bitcast_fusion
  691.4 0.7 copy.7
  692.0 1.5 sub.27
  693.5 0.2 abs_reduce_fusion
  693.8 0.0 copy-start.1
  693.8 1.1 broadcast_divide_fusion
  694.9 0.0 copy-done.1
  (3 shorter events, 0.0 us)
Async XLA Ops:
  667.7 23.6 %copy-start = (f32[4,2,256,128]{3,2,1,0:T(8,128)S(1)}, f32[4,2,256,128]{3,2,1,0:T(8,128)}, u32[]{:S(2)}) copy-start(f32[4,2,256,128]{3,2,1,0:T(8,128)} %get-tuple-element.7) | copy-start | bytes 3145732
  693.8 1.1 copy-start.1
where the time goes:
time: 696 us; the launch traced here: 695 us
  Pallas kernels  685 us (98%)
    pallas_call x1, Pallas kernels, per_device(): pl.pallas_call(functools.partial(exchange, sizes), out_shape=(jax.ShapeDt...  638 us
    pallas_call x1, Pallas kernels, pick_slots(): pl.pallas_call(copy_block, grid_spec=pltpu.PrefetchScalarGridSpec(num_sca...  24.2 us
    pallas_call x1, Pallas kernels, settle(): pl.pallas_call(copy_block, grid=(total // rows,), in_specs=[pl.BlockSpec(...  23.6 us

commit v1 on v0

v1 whole, which is shorter than its diff:
```python
import functools
import math

import jax
import jax.numpy as jnp
import numpy as np
from jax import lax
from jax.experimental import pallas as pl
from jax.experimental.pallas import tpu as pltpu
from jax.sharding import PartitionSpec as P

LEVELS = [
    -1.0,
    -0.6961928009986877,
    -0.5250730514526367,
    -0.39491748809814453,
    -0.28444138169288635,
    -0.18477343022823334,
    -0.09105003625154495,
    0.0,
    0.07958029955625534,
    0.16093020141124725,
    0.24611230194568634,
    0.33791524171829224,
    0.44070982933044434,
    0.5626170039176941,
    0.7229568362236023,
    1.0,
]
MIDPOINTS = [(LEVELS[k] + LEVELS[k + 1]) / 2.0 for k in range(15)]
STEPSIZES = [LEVELS[k + 1] - LEVELS[k] for k in range(15)]
EPS = 1e-06
LANES = 128
BLOCK = 64
MESH = pl.DeviceIdType.MESH


def reached_levels():
    total = np.float32(LEVELS[0])
    reached = [float(total)]
    for step in STEPSIZES:
        total = np.float32(total + np.float32(step))
        reached.append(float(total))
    return reached


REACHED = reached_levels()


def code_tile(w):
    lane = lax.broadcasted_iota(jnp.int32, w.shape, 1)
    top = jnp.abs(w)
    low = lane < BLOCK
    first = jnp.broadcast_to(jnp.max(jnp.where(low, top, 0.0), axis=1, keepdims=True), w.shape)
    second = jnp.broadcast_to(jnp.max(jnp.where(low, 0.0, top), axis=1, keepdims=True), w.shape)
    spread = jnp.where(lane < BLOCK, first, second)
    ratio = w / (spread + EPS)
    level = jnp.full(w.shape, REACHED[0], jnp.float32)
    for middle, value in zip(MIDPOINTS, REACHED[1:]):
        level = jnp.where(ratio > middle, value, level)
    return spread * level, first, second


def exchange(
    sizes, loader_owner, slab_order, sectioned, out, kept, scales, peaks, sums, arrive, ld, pick, snd, own, stage,
    coded, tops, mine, ours, got, met, slots, origin, ls, s1, r1, s2, r2, sa, ra, sm, rm, so, ro,
):
    owners, tp, slab_rows, rows, pieces, per_block, columns, ahead, loads, sends, codes = sizes
    t = lax.axis_index("tp")
    f = lax.axis_index("fsdp")
    width = columns // pieces
    tiles = width // LANES
    chunks = slab_rows // rows * pieces

    def row_span(c):
        return pl.ds(pl.multiple_of(c // pieces * rows, rows), rows)

    def column_span(c):
        return pl.ds(pl.multiple_of(lax.rem(c, pieces) * width, LANES), width)

    def load(c):
        slot = lax.rem(c, loads)
        return pltpu.make_async_copy(sectioned.at[:, row_span(c), column_span(c)], ld.at[slot], ls.at[slot])

    for c in range(min(loads, chunks)):
        load(c).start()

    barrier = pltpu.get_barrier_semaphore()
    for d in range(1, owners):
        pl.semaphore_signal(barrier, inc=1, device_id={"fsdp": lax.rem(f + d, owners)}, device_id_type=MESH)
    for e in range(1, tp):
        pl.semaphore_signal(barrier, inc=1, device_id={"tp": lax.rem(t + e, tp)}, device_id_type=MESH)

    def find_slot(d, _):
        to = lax.rem(f + d, owners)

        def look(p, found):
            s = (p // per_block * owners + to) * per_block + lax.rem(p, per_block)
            return jnp.where(loader_owner[s] == f, slab_order[s], found)

        slots[d] = lax.fori_loop(0, owners, look, 0)
        origin[d] = loader_owner[(d // per_block * owners + f) * per_block + lax.rem(d, per_block)]
        return 0

    lax.fori_loop(0, owners, find_slot, 0)
    mine[...] = jnp.zeros_like(mine)
    peaks[...] = jnp.zeros_like(peaks)
    tops[...] = jnp.zeros_like(tops)
    pl.semaphore_wait(barrier, owners - 1 + tp - 1)

    def first_hop(c, d):
        slot = lax.rem(c, sends)
        return pltpu.make_async_remote_copy(
            src_ref=snd.at[slot, d - 1],
            dst_ref=arrive.at[c, f],
            send_sem=s1.at[slot],
            recv_sem=r1.at[c],
            device_id={"fsdp": lax.rem(f + d, owners)},
            device_id_type=MESH,
        )

    def first_sent(slot):
        whole = snd.at[slot]
        pltpu.make_async_copy(whole, whole, s1.at[slot]).wait()

    def first_landed(c):
        whole = arrive.at[c, pl.ds(0, owners - 1)]
        pltpu.make_async_copy(whole, whole, r1.at[c]).wait()

    low = lax.broadcasted_iota(jnp.int32, (rows, LANES), 1) < BLOCK

    def push(c):
        load(c).wait()

        @pl.when(c >= sends)
        def _():
            first_sent(lax.rem(c, sends))

        def take(o, _):
            pick[o] = ld[lax.rem(c, loads), o]
            return 0

        lax.fori_loop(0, owners, take, 0)

        @pl.when(c + loads < chunks)
        def _():
            load(c + loads).start()

        def choose(d, _):
            snd[lax.rem(c, sends), d - 1] = pick[slots[d]]
            return 0

        lax.fori_loop(1, owners, choose, 0)
        own[lax.rem(c, sends)] = pick[slots[0]]
        for d in order(owners):
            first_hop(c, d).start()

        def add(o, _):
            w = jnp.abs(pick[o].astype(jnp.float32))
            total = jnp.zeros((rows, LANES), jnp.float32)
            for j in range(tiles):
                top = w[:, j * LANES : (j + 1) * LANES]
                first = jnp.max(jnp.where(low, top, 0.0), axis=1, keepdims=True)
                second = jnp.max(jnp.where(low, 0.0, top), axis=1, keepdims=True)
                total = total + jnp.broadcast_to(first + second, total.shape)
            mine[...] += total
            return 0

        lax.fori_loop(0, owners, add, 0)

    def second_hop(c, e):
        slot = lax.rem(c, codes)
        return pltpu.make_async_remote_copy(
            src_ref=coded.at[slot, e - 1],
            dst_ref=out.at[e - 1, :, row_span(c), column_span(c)],
            send_sem=s2.at[slot],
            recv_sem=r2.at[c],
            device_id={"tp": lax.rem(t + e, tp)},
            device_id_type=MESH,
        )

    def second_sent(slot):
        whole = coded.at[slot]
        pltpu.make_async_copy(whole, whole, s2.at[slot]).wait()

    def second_landed(c):
        whole = coded.at[0]
        pltpu.make_async_copy(whole, whole, r2.at[c]).wait()

    def top_hop(r, e):
        span = pl.ds(pl.multiple_of(r * rows, rows), rows)
        return pltpu.make_async_remote_copy(
            src_ref=tops.at[e - 1, :, span],
            dst_ref=scales.at[e - 1, :, span],
            send_sem=sa.at[r],
            recv_sem=ra.at[r],
            device_id={"tp": lax.rem(t + e, tp)},
            device_id_type=MESH,
        )

    def top_done(r, sem):
        span = pl.ds(pl.multiple_of(r * rows, rows), rows)
        whole = tops.at[:, :, span]
        pltpu.make_async_copy(whole, whole, sem.at[r]).wait()

    def code(c, e):
        lane = lax.broadcasted_iota(jnp.int32, (rows, LANES), 1)
        to = lax.rem(t + e, tp)
        start = lax.rem(c, pieces) * (2 * tiles)

        def place(k, _):
            w = stage[origin[to * per_block + k]].astype(jnp.float32)
            if e < tp:
                held = tops[e - 1, k, row_span(c), :]
            else:
                held = peaks[k, row_span(c), :]
            made = []
            for j in range(tiles):
                value, first, second = code_tile(w[:, j * LANES : (j + 1) * LANES])
                made.append(value.astype(jnp.bfloat16))
                index = start + 2 * j
                held = jnp.where(lane == index, first, jnp.where(lane == index + 1, second, held))
            made = jnp.concatenate(made, axis=1)
            if e < tp:
                coded[lax.rem(c, codes), e - 1, k] = made
                tops[e - 1, k, row_span(c), :] = held
            else:
                kept[k, row_span(c), column_span(c)] = made
                peaks[k, row_span(c), :] = held
            return 0

        lax.fori_loop(0, per_block, place, 0)

    def sum_hop(d):
        return pltpu.make_async_remote_copy(
            src_ref=mine,
            dst_ref=got.at[d],
            send_sem=sm.at[d],
            recv_sem=rm.at[d],
            device_id={"fsdp": lax.rem(f + d, owners)},
            device_id_type=MESH,
        )

    def sum_turn(e):
        return pltpu.make_async_remote_copy(
            src_ref=ours,
            dst_ref=met.at[e],
            send_sem=so.at[e],
            recv_sem=ro.at[e],
            device_id={"tp": lax.rem(t + e, tp)},
            device_id_type=MESH,
        )

    def start_sums():
        for d in range(1, owners):
            sum_hop(d).start()

    def prime(c, _):
        push(c)
        return 0

    lax.fori_loop(0, ahead, prime, 0)
    if ahead == chunks:
        start_sums()

    def chunk(c, _):
        @pl.when(c + ahead < chunks)
        def _():
            push(c + ahead)

        if ahead < chunks:

            @pl.when(c + ahead == chunks - 1)
            def _():
                start_sums()

        first_landed(c)

        def take(d, _):
            o = lax.rem(f + d, owners)
            stage[o] = arrive[c, o]
            return 0

        lax.fori_loop(1, owners, take, 0)
        stage[f] = own[lax.rem(c, sends)]

        @pl.when(c >= codes)
        def _():
            second_sent(lax.rem(c, codes))

        for e in range(1, tp + 1):
            code(c, e)
            if e < tp:
                second_hop(c, e).start()

        @pl.when(lax.rem(c, pieces) == pieces - 1)
        def _():
            for e in range(1, tp):
                top_hop(c // pieces, e).start()

        return 0

    lax.fori_loop(0, chunks, chunk, 0)

    for d in range(1, owners):
        sum_hop(d).wait()
    total = mine[...]
    for d in range(1, owners):
        total = total + got[d]
    ours[...] = total
    for e in range(1, tp):
        sum_turn(e).start()
    for c in range(max(chunks - sends, 0), chunks):
        first_sent(c % sends)
    for c in range(max(chunks - codes, 0), chunks):
        second_sent(c % codes)

    def settle_tops(r, _):
        top_done(r, sa)
        top_done(r, ra)
        return 0

    lax.fori_loop(0, chunks // pieces, settle_tops, 0)

    def finish(c, _):
        second_landed(c)
        return 0

    lax.fori_loop(0, chunks, finish, 0)
    for e in range(1, tp):
        sum_turn(e).wait()
    total = ours[...]
    for e in range(1, tp):
        total = total + met[e]
    sums[...] = total


def order(owners):
    middle = owners // 2
    return sorted(range(1, owners), key=lambda d: (abs(d - middle), d))


def place_out(sizes, coded, kept, scales, peaks, sums, out, codes_out, tops_out, codes, spread, table, sem, sent):
    blocks, entries, count = sizes
    per_block, slab_rows, width = kept.shape
    tp = table.shape[0]
    me = lax.axis_index("tp")
    group = 256
    copies = []
    for e in range(tp):
        t = lax.rem(me + tp - e, tp)
        band = out.at[:, :, pl.ds(pl.multiple_of(t * width, LANES), width)]
        copies.append(pltpu.make_async_copy(coded.at[e - 1] if e else kept, band, sem.at[e]))
        copies[-1].start()
    for e in range(tp):
        table[lax.rem(me + tp - e, tp)] = scales[e - 1] if e else peaks[...]

    step = math.gcd(entries, group)
    period, turns = group // step, entries // step
    height = per_block * slab_rows // period
    lane = lax.broadcasted_iota(jnp.int32, (height, LANES), 1)
    offset = jnp.sum(sums[...], axis=0, keepdims=True) / count

    columns = [None] * (2 * turns)

    def lay(at, value):
        columns[at] = value if columns[at] is None else columns[at] + value

    def emit(j):
        left = columns[2 * j] - offset
        right = columns[2 * j + 1] - offset
        largest = jnp.maximum(jnp.abs(left), jnp.abs(right))
        largest = jnp.broadcast_to(jnp.max(largest, axis=1, keepdims=True), left.shape)
        scale = largest + EPS
        rows = pl.ds(j, height, stride=turns)
        codes[0, rows, :] = left / scale
        codes[1, rows, :] = right / scale
        spread[rows, :] = largest

    done = 0
    for i in range(period):
        for t in range(tp):
            piece = table[t, pl.ds(i, height, stride=period), :]
            at, shift = divmod(i * entries + t * blocks, LANES)
            if shift:
                piece = pltpu.roll(piece, shift, 1)
                lay(at, jnp.where(lane >= shift, piece, 0.0))
                if shift + blocks > LANES:
                    lay(at + 1, jnp.where(lane < shift, piece, 0.0))
            else:
                lay(at, piece)
            filled = (i * entries + (t + 1) * blocks) // group
            while done < filled:
                emit(done)
                done += 1

    row = lax.broadcasted_iota(jnp.int32, (LANES, LANES), 0)
    diagonal = row == lax.broadcasted_iota(jnp.int32, (LANES, LANES), 1)
    total = codes.shape[1]
    for s in range(total // LANES + (total % LANES > 0)):
        size = min(LANES, total - s * LANES)
        part = jnp.where(diagonal[:size], spread[s * LANES : s * LANES + size, :], 0.0)
        tops_out[s : s + 1, :] = jnp.sum(part, axis=0, keepdims=True)
    for h in range(2):
        copies.append(pltpu.make_async_copy(codes.at[h], codes_out.at[:, pl.ds(h * LANES, LANES)], sent.at[h]))
        copies[-1].start()
    for copy in copies:
        copy.wait()


def per_device(sectioned, loader_owner, slab_order):
    owners = lax.axis_size("fsdp")
    tp = lax.axis_size("tp")
    slots, slab_rows, columns = sectioned.shape
    slab_count = loader_owner.shape[0]
    per_block = owners // tp
    rows = min(16, slab_rows)
    groups = columns // LANES
    pieces = next(p for p in (4, 2, 1) if groups % p == 0)
    width = columns // pieces
    chunks = slab_rows // rows * pieces
    ahead = min(8, chunks)
    loads, sends, codes = 2, min(ahead + 2, chunks), min(3, chunks)
    blocks = columns // BLOCK
    sizes = (owners, tp, slab_rows, rows, pieces, per_block, columns, ahead, loads, sends, codes)
    dma = pltpu.SemaphoreType.DMA
    anywhere = pl.BlockSpec(memory_space=pl.ANY)
    vmem = pl.BlockSpec(memory_space=pltpu.VMEM)
    smem = pl.BlockSpec(memory_space=pltpu.SMEM)
    half, full = jnp.bfloat16, jnp.float32
    buffers = [
        ((chunks, owners, rows, width), half),
        ((loads, owners, rows, width), half),
        ((owners, rows, width), half),
        ((sends, owners - 1, rows, width), half),
        ((sends, rows, width), half),
        ((owners, rows, width), half),
        ((codes, tp - 1, per_block, rows, width), half),
        ((tp - 1, per_block, slab_rows, LANES), full),
        ((rows, LANES), full),
        ((rows, LANES), full),
        ((owners, rows, LANES), full),
        ((tp, rows, LANES), full),
    ]
    held = sum(int(np.prod(shape)) * jnp.dtype(kind).itemsize for shape, kind in buffers)
    coded, kept, scales, peaks, sums = pl.pallas_call(
        functools.partial(exchange, sizes),
        out_shape=(
            pltpu.VMEM((tp - 1, per_block, slab_rows, columns), half),
            pltpu.VMEM((per_block, slab_rows, columns), half),
            pltpu.VMEM((tp - 1, per_block, slab_rows, LANES), full),
            pltpu.VMEM((per_block, slab_rows, LANES), full),
            pltpu.VMEM((rows, LANES), full),
        ),
        in_specs=[smem, smem, anywhere],
        out_specs=(vmem,) * 5,
        scratch_shapes=[pltpu.VMEM(shape, kind) for shape, kind in buffers]
        + [
            pltpu.SMEM((owners,), jnp.int32),
            pltpu.SMEM((owners,), jnp.int32),
            dma((loads,)),
            dma((sends,)),
            dma((chunks,)),
            dma((codes,)),
            dma((chunks,)),
            dma((chunks // pieces,)),
            dma((chunks // pieces,)),
            dma((owners,)),
            dma((owners,)),
            dma((tp,)),
            dma((tp,)),
        ],
        compiler_params=pltpu.CompilerParams(
            collective_id=0, has_side_effects=True, vmem_limit_bytes=held + 3 * 2**19
        ),
        name="exchange",
    )(loader_owner, slab_order, sectioned)
    entries = tp * blocks
    total = per_block * slab_rows * entries // 256
    lines = -(-total // LANES)
    dequant, scale_codes, tops = pl.pallas_call(
        functools.partial(place_out, (blocks, entries, float(slab_count * slab_rows * entries))),
        out_shape=(
            jax.ShapeDtypeStruct((per_block, slab_rows, tp * columns), half),
            jax.ShapeDtypeStruct((total, 2 * LANES), full),
            jax.ShapeDtypeStruct((lines, LANES), full),
        ),
        in_specs=[vmem] * 5,
        out_specs=(anywhere, anywhere, vmem),
        scratch_shapes=[
            pltpu.VMEM((2, total, LANES), full),
            pltpu.VMEM((total, LANES), full),
            pltpu.VMEM((tp, per_block * slab_rows, LANES), full),
            dma((tp,)),
            dma((2,)),
        ],
        compiler_params=pltpu.CompilerParams(vmem_limit_bytes=7 * 2**19),
        name="place_out",
    )(coded, kept, scales.reshape(tp - 1, -1, LANES), peaks.reshape(-1, LANES), sums)
    dequant = dequant.reshape(per_block * slab_rows, tp * columns)
    return (dequant, scale_codes, tops.reshape(-1)[:total])


def solution(mesh):
    return jax.shard_map(
        per_device,
        mesh=mesh,
        in_specs=(P("fsdp", None, "tp"), P(), P()),
        out_specs=(P(("tp", "fsdp"), None), P(("tp", "fsdp"), None), P(("tp", "fsdp"))),
        check_vma=False,
    )
```

time: 696 us -> 616 us (0.89)
  Pallas kernels: 685 us -> 615 us
    pallas_call x3 -> x2, Pallas kernels: 685 us -> 615 us  [the longest x1 604 us: per_device(): pl.pallas_call(functools.partial(exchange, sizes), out_shape=(pltpu.VMEM(...]
where the time goes in v1:
time: 616 us
  Pallas kernels  615 us (100%)
    pallas_call x1, Pallas kernels, per_device(): pl.pallas_call(functools.partial(exchange, sizes), out_shape=(pltpu.VMEM(...  604 us

profile of v1, /device:TPU:13, one launch (start us, length us, event | category | flops | bytes accessed | tf_op | source)
XLA Modules:
  0.0 615.7 jit_solution(15199550857220483819)
XLA Ops:
  0.6 604.3 %exchange.1 = (bf16[3,2,256,6656]{3,2,1,0:T(8,128)(2,1)S(1)}, bf16[2,256,6656]{2,1,0:T(8,128)(2,1)S(1)}, f32[3,2,256,128]{3,2,1,0:T(8,128)S(1)}, f32[2,256,128]{2,1,0:T(8,128)S(1)}, f32[16,128]{1,0:T(8,128)S(1)}) custom-call(s32[64]{0:T(128)} %loader_owner.1, s32[64]{0:T(128)} %slab_order.1, bf16[8,256,6656]{2,1,0:T(8,128)(2,1)} %sectioned.1), custom_call_target="tpu_custom_call" | custom-call | tf_op jit(solution)/shard_map/exchange/pallas_call | solution.py:446
  604.9 10.8 %place_out.1 = (bf16[2,256,26624]{2,1,0:T(8,128)(2,1)}, f32[832,256]{1,0:T(8,128)}, f32[7,128]{1,0:T(8,128)}) custom-call(bf16[3,2,256,6656]{3,2,1,0:T(8,128)(2,1)S(1)} %get-tuple-element.11.coded, bf16[2,256,6656]{2,1,0:T(8,128)(2,1)S(1)} %get-tuple-element.12.kept, f32[3,512,128]{2,1,0:T(8,128)S(1)} %bitcast.5, f32[512,128]{1,0:T(8,128)S(1)} %bitcast.6, ...), custom_call_target="tpu_custom_call" | custom-call | tf_op jit(solution)/shard_map/place_out/pallas_call | solution.py:481

commit v2 on v1

--- a/solution.py
+++ b/solution.py
@@ -340,7 +340,7 @@
     return sorted(range(1, owners), key=lambda d: (abs(d - middle), d))
 
 
-def place_out(sizes, coded, kept, scales, peaks, sums, out, codes_out, tops_out, codes, spread, table, sem, sent):
+def place_out(sizes, coded, kept, scales, peaks, sums, out, codes_out, tops_out, codes, spread, table, peak_lines, sem, sent):
     blocks, entries, count = sizes
     per_block, slab_rows, width = kept.shape
     tp = table.shape[0]
@@ -350,8 +350,10 @@
     for e in range(tp):
         t = lax.rem(me + tp - e, tp)
         band = out.at[:, :, pl.ds(pl.multiple_of(t * width, LANES), width)]
-        copies.append(pltpu.make_async_copy(coded.at[e - 1] if e else kept, band, sem.at[e]))
-        copies[-1].start()
+        whole = coded.at[e - 1] if e else kept
+        for k in range(per_block):
+            copies.append(pltpu.make_async_copy(whole.at[k], band.at[k], sem.at[e, k]))
+            copies[-1].start()
     for e in range(tp):
         table[lax.rem(me + tp - e, tp)] = scales[e - 1] if e else peaks[...]
 
@@ -400,7 +402,9 @@
     for s in range(total // LANES + (total % LANES > 0)):
         size = min(LANES, total - s * LANES)
         part = jnp.where(diagonal[:size], spread[s * LANES : s * LANES + size, :], 0.0)
-        tops_out[s : s + 1, :] = jnp.sum(part, axis=0, keepdims=True)
+        peak_lines[s : s + 1, :] = jnp.sum(part, axis=0, keepdims=True)
+    copies.append(pltpu.make_async_copy(peak_lines, tops_out, sent.at[2]))
+    copies[-1].start()
     for h in range(2):
         copies.append(pltpu.make_async_copy(codes.at[h], codes_out.at[:, pl.ds(h * LANES, LANES)], sent.at[h]))
         copies[-1].start()
@@ -419,7 +423,7 @@
     pieces = next(p for p in (4, 2, 1) if groups % p == 0)
     width = columns // pieces
     chunks = slab_rows // rows * pieces
-    ahead = min(8, chunks)
+    ahead = min(3, chunks)
     loads, sends, codes = 2, min(ahead + 2, chunks), min(3, chunks)
     blocks = columns // BLOCK
     sizes = (owners, tp, slab_rows, rows, pieces, per_block, columns, ahead, loads, sends, codes)
@@ -486,13 +490,14 @@
             jax.ShapeDtypeStruct((lines, LANES), full),
         ),
         in_specs=[vmem] * 5,
-        out_specs=(anywhere, anywhere, vmem),
+        out_specs=(anywhere,) * 3,
         scratch_shapes=[
             pltpu.VMEM((2, total, LANES), full),
             pltpu.VMEM((total, LANES), full),
             pltpu.VMEM((tp, per_block * slab_rows, LANES), full),
-            dma((tp,)),
-            dma((2,)),
+            pltpu.VMEM((lines, LANES), full),
+            dma((tp, per_block)),
+            dma((3,)),
         ],
         compiler_params=pltpu.CompilerParams(vmem_limit_bytes=7 * 2**19),
         name="place_out",

time: 616 us -> 614 us (level)
  no operation moved by 1% of the time
where the time goes in v2:
time: 614 us
  Pallas kernels  613 us (100%)
    pallas_call x1, Pallas kernels, per_device(): pl.pallas_call(functools.partial(exchange, sizes), out_shape=(pltpu.VMEM(...  603 us

profile of v2, /device:TPU:13, one launch (start us, length us, event | category | flops | bytes accessed | tf_op | source)
XLA Modules:
  0.0 613.9 jit_solution(12434336979199836153)
XLA Ops:
  0.6 602.8 %exchange.1 = (bf16[3,2,256,6656]{3,2,1,0:T(8,128)(2,1)S(1)}, bf16[2,256,6656]{2,1,0:T(8,128)(2,1)S(1)}, f32[3,2,256,128]{3,2,1,0:T(8,128)S(1)}, f32[2,256,128]{2,1,0:T(8,128)S(1)}, f32[16,128]{1,0:T(8,128)S(1)}) custom-call(s32[64]{0:T(128)} %loader_owner.1, s32[64]{0:T(128)} %slab_order.1, bf16[8,256,6656]{2,1,0:T(8,128)(2,1)} %sectioned.1), custom_call_target="tpu_custom_call" | custom-call | tf_op jit(solution)/shard_map/exchange/pallas_call | solution.py:450
  603.4 10.4 %place_out.1 = (bf16[2,256,26624]{2,1,0:T(8,128)(2,1)}, f32[832,256]{1,0:T(8,128)}, f32[7,128]{1,0:T(8,128)}) custom-call(bf16[3,2,256,6656]{3,2,1,0:T(8,128)(2,1)S(1)} %get-tuple-element.11.coded, bf16[2,256,6656]{2,1,0:T(8,128)(2,1)S(1)} %get-tuple-element.12.kept, f32[3,512,128]{2,1,0:T(8,128)S(1)} %bitcast.5, f32[512,128]{1,0:T(8,128)S(1)} %bitcast.6, ...), custom_call_target="tpu_custom_call" | custom-call | tf_op jit(solution)/shard_map/place_out/pallas_call | solution.py:485
